TPU v7x, 256 devices: a whole 4x4x8 slice. The times are simulated.
256 devices in a mesh: row: 16 (over x, z_hi), col: 16 (over y, z_lo, core).
Axes of the slice: x: 4, y: 4, z: 8 (z_hi: 4, z_lo: 2; z = z_hi * 2 + z_lo), core: 2. Of those that a mesh axis runs over, the one named last changes fastest.
Arguments:
- tokens: bfloat16 [2048, 8192], P('col', 'row'), may hold values from -6 to 6
- grad_out: bfloat16 [2048, 8192], P('col', 'row'), may hold values from -2 to 2
- gate: bfloat16 [2048, 14336], P('row', 'col'), may hold values from -6 to 6
- up: bfloat16 [2048, 14336], P('row', 'col'), may hold values from -6 to 6
- gate_weight: bfloat16 [8192, 14336], P('row', 'col'), may hold values from -0.0625 to 0.0625
- up_weight: bfloat16 [8192, 14336], P('row', 'col'), may hold values from -0.0625 to 0.0625
- down_weight: bfloat16 [8192, 14336], P('row', 'col'), may hold values from -0.046875 to 0.046875
Outputs:
- grad_tokens: bfloat16 [2048, 8192], P('col', 'row')
- grad_gate_weight: float32 [8192, 14336], P('row', 'col')
- grad_up_weight: float32 [8192, 14336], P('row', 'col')
- grad_down_weight: float32 [8192, 14336], P('row', 'col')
All inputs are finite; a program needn't handle non-finite values.
Results may differ from a plain program's by a relative error of at most 0.0049.
Values may be sent and summed in bfloat16 or wider, within the bound.
A program may use at most 128 MiB of HBM per device.

v0:
```python
import jax
import jax.numpy as jnp
from jax import lax
from jax.sharding import Mesh
from jax.sharding import PartitionSpec as P

ROW = ("row_0", "row_1")


def side_by_side(arrays, axis, dim, along):
    both = jnp.concatenate(arrays, axis=along)
    whole, at, finished = (lax.all_gather(both, axis, axis=dim, tiled=True), 0, [])
    for a in arrays:
        finished.append(lax.slice_in_dim(whole, at, at + a.shape[along], axis=along))
        at += a.shape[along]
    return tuple(finished)


def own_rows(subtotal, axes):
    for axis in axes:
        subtotal = lax.psum_scatter(subtotal, axis, scatter_dimension=0, tiled=True)
    return subtotal


def cut_along(shard, dim, size):
    lengths = shard.shape
    blocks = shard.reshape(*lengths[:dim], size, lengths[dim] // size, *lengths[dim + 1 :])
    return jnp.moveaxis(blocks, dim, 0)


def sum_at_owner(shard, axis, dim):
    blocks = cut_along(shard, dim, lax.axis_size(axis))
    arrived = lax.all_to_all(blocks, axis, split_axis=0, concat_axis=0, tiled=True)
    return arrived.sum(axis=0)


def backward_swiglu(grad_hidden, gate, up):
    gate32 = gate.astype(jnp.float32)
    up32 = up.astype(jnp.float32)
    sigma = jax.nn.sigmoid(gate32)
    active = gate32 * sigma
    hidden = (active * up32).astype(jnp.bfloat16)
    grad_up = (grad_hidden * active).astype(jnp.bfloat16)
    grad_gate = (grad_hidden * up32 * sigma * (1.0 + gate32 * (1.0 - sigma))).astype(jnp.bfloat16)
    return (hidden, grad_gate, grad_up)


def per_device(tokens, grad_out, gate, up, gate_weight, up_weight, down_weight):
    tokens_all, grad_all = side_by_side((tokens, grad_out), "col", 0, 1)
    grad_hidden = own_rows(jnp.dot(grad_all, down_weight, preferred_element_type=jnp.float32), ROW)
    local_parts = backward_swiglu(grad_hidden, gate, up)
    hidden, grad_gate, grad_up = side_by_side(
        (local_parts[0], local_parts[1], local_parts[2]), ROW, 0, 1
    )
    inner = (((1,), (1,)), ((), ()))
    first = lax.dot_general(grad_gate, gate_weight, inner, preferred_element_type=jnp.float32)
    grad_tokens = sum_at_owner(
        first + lax.dot_general(grad_up, up_weight, inner, preferred_element_type=jnp.float32),
        "col",
        0,
    )
    outer = (((0,), (0,)), ((), ()))
    grad_down_weight = lax.dot_general(grad_all, hidden, outer, preferred_element_type=jnp.float32)
    stacked = jnp.concatenate([grad_gate, grad_up], axis=1)
    both_grads = lax.dot_general(tokens_all, stacked, outer, preferred_element_type=jnp.float32)
    width = grad_gate.shape[1]
    grad_gate_weight = both_grads[:, :width]
    grad_up_weight = both_grads[:, width:]
    return (grad_tokens.astype(jnp.bfloat16), grad_gate_weight, grad_up_weight, grad_down_weight)


def solution(mesh):
    finer = Mesh(mesh.devices.reshape(4, 4, mesh.shape["col"]), ("row_0", "row_1", "col"))
    placed = (
        P("col", ROW),
        P("col", ROW),
        P(ROW, "col"),
        P(ROW, "col"),
        P(ROW, "col"),
        P(ROW, "col"),
        P(ROW, "col"),
    )
    return jax.shard_map(
        per_device,
        mesh=finer,
        in_specs=placed,
        out_specs=(P("col", ROW), P(ROW, "col"), P(ROW, "col"), P(ROW, "col")),
        check_vma=False,
    )
```

profile of v0, /device:TPU:36, one launch (start us, length us, event | category | flops | bytes accessed | tf_op | source)
XLA Modules:
  0.0 401.5 jit_solution(10449779445076223142)
XLA Ops:
  7.2 0.0 copy-start
  7.2 0.0 all-gather.3.cloned.1.call-start
  7.2 1.8 pad_maximum_fusion.1
  9.0 0.0 all-gather.3.cloned.1.call-update
  9.0 0.0 reduce-scatter.3.cloned.1.call-start
  9.1 43.3 %all-gather.3.cloned.1.call-done = bf16[2048,1024]{1,0:T(8,128)(2,1)} async-done(((bf16[128,1024]{1,0:T(8,128)(2,1)}), bf16[2048,1024]{1,0:T(8,128)(2,1)}) %all-gather.3.cloned.1.call-update) | async-done | bytes 4194320 | tf_op jit(solution)/shard_map/all_gather | solution.py:12
  52.4 0.0 copy-done
  52.4 6.9 %fusion.13 = f32[2048,896]{1,0:T(8,128)} fusion(bf16[512,896]{1,0:T(8,128)(2,1)S(1)} %copy-done, bf16[2048,1024]{1,0:T(8,128)(2,1)} %all-gather.3.cloned.1.call-done), kind=kOutput, calls=%fused_computation.11 | convolution fusion | flops 1879048192 | bytes 10354688 | tf_op jit(solution)/shard_map/dot_general | solution.py:50
  59.3 0.0 copy-start.1
  59.3 0.0 copy-start.2
  59.3 0.0 reduce-scatter.3.cloned.1.call-update
  59.3 0.0 copy-start.5
  59.3 0.0 reduce-scatter.5.cloned.1.call-start
  59.4 74.1 %reduce-scatter.3.cloned.1.call-done = f32[512,896]{1,0:T(8,128)} async-done(((f32[2048,896]{1,0:T(8,128)}), f32[512,896]{1,0:T(8,128)}) %reduce-scatter.3.cloned.1.call-update) | async-done | bytes 1835024 | tf_op jit(solution)/shard_map/reduce_scatter | solution.py:21
  133.4 0.0 reduce-scatter.5.cloned.1.call-update
  133.5 0.0 all-gather.5.cloned.1.call-start
  133.5 48.5 %reduce-scatter.5.cloned.1.call-done = f32[128,896]{1,0:T(8,128)} async-done(((f32[512,896]{1,0:T(8,128)}), f32[128,896]{1,0:T(8,128)}) %reduce-scatter.5.cloned.1.call-update) | async-done | bytes 458768 | tf_op jit(solution)/shard_map/reduce_scatter | solution.py:21
  182.0 0.0 copy-done.1
  182.0 0.0 copy-done.2
  182.0 1.3 fusion.18
  183.3 0.9 pad_maximum_fusion
  184.2 0.0 all-gather.5.cloned.1.call-update
  184.2 0.0 copy-start.6
  184.2 142.8 %all-gather.5.cloned.1.call-done = bf16[2048,2688]{1,0:T(8,128)(2,1)} async-done(((bf16[128,2688]{1,0:T(8,128)(2,1)}), bf16[2048,2688]{1,0:T(8,128)(2,1)}) %all-gather.5.cloned.1.call-update) | async-done | bytes 11010064 | tf_op jit(solution)/shard_map/all_gather | solution.py:12
  327.0 0.0 copy-done.5
  327.0 0.0 copy-start.3
  327.0 4.6 %fusion.4 = f32[2048,512]{1,0:T(8,128)S(1)} fusion(bf16[512,896]{1,0:T(8,128)(2,1)S(1)} %copy-done.5, bf16[2048,2688]{1,0:T(8,128)(2,1)} %all-gather.5.cloned.1.call-done), kind=kOutput, calls=%fused_computation.4 | convolution fusion | flops 1879048192 | bytes 8781824 | tf_op jit(solution)/shard_map/dot_general | solution.py:58
  331.6 0.0 copy-done.6
  331.6 0.7 copy-done.3
  332.3 4.4 %fusion.8 = f32[2048,512]{1,0:T(8,128)} fusion(f32[2048,512]{1,0:T(8,128)S(1)} %fusion.4, bf16[512,896]{1,0:T(8,128)(2,1)S(1)} %copy-done.6, bf16[2048,2688]{1,0:T(8,128)(2,1)S(1)} %copy-done.3), kind=kOutput, calls=%fused_computation.8 | convolution fusion | flops 1880096768 | bytes 12976128 | tf_op jit(solution)/shard_map/dot_general | solution.py:56
  336.7 5.7 %all-to-all-start = ((f32[16,128,512]{2,1,0:T(8,128)}), f32[16,128,512]{2,1,0:T(8,128)}, u32[]{:S(2)}, u32[]{:S(2)}) async-start(f32[16,128,512]{2,1,0:T(8,128)} %bitcast.4), calls=%async_computation.2 | async-start | bytes 8388608 | tf_op jit(solution)/shard_map/all_to_all | solution.py:33
  342.5 8.0 %fusion = f32[512,1792]{1,0:T(8,128)S(1)} fusion(bf16[2048,2688]{1,0:T(8,128)(2,1)} %all-gather.5.cloned.1.call-done, bf16[2048,1024]{1,0:T(8,128)(2,1)} %all-gather.3.cloned.1.call-done), kind=kOutput, calls=%fused_computation | convolution fusion | flops 3758096384 | bytes 13107200 | tf_op jit(solution)/shard_map/dot_general | solution.py:65
  350.4 0.0 copy-start.4
  350.4 2.1 fusion.23
  352.5 1.4 copy-done.4
  353.9 5.7 %fusion.2 = f32[512,896]{1,0:T(8,128)} fusion(bf16[2048,2688]{1,0:T(8,128)(2,1)} %all-gather.5.cloned.1.call-done, bf16[2048,1024]{1,0:T(8,128)(2,1)S(1)} %copy-done.4), kind=kOutput, calls=%fused_computation.2 | convolution fusion | flops 1879048192 | bytes 7602176 | tf_op jit(solution)/shard_map/dot_general | solution.py:63
  359.6 32.0 %all-to-all-done = f32[16,128,512]{2,1,0:T(8,128)} async-done(((f32[16,128,512]{2,1,0:T(8,128)}), f32[16,128,512]{2,1,0:T(8,128)}, u32[]{:S(2)}, u32[]{:S(2)}) %all-to-all-start) | async-done | bytes 4194336 | tf_op jit(solution)/shard_map/all_to_all | solution.py:33
  391.6 3.3 reduce_sum.9
Async XLA Ops:
  7.2 45.2 %copy-start = (bf16[512,896]{1,0:T(8,128)(2,1)S(1)}, bf16[512,896]{1,0:T(8,128)(2,1)}, u32[]{:S(2)}) copy-start(bf16[512,896]{1,0:T(8,128)(2,1)} %param.13) | copy-start | bytes 2752516
  7.2 45.2 %all-gather.3.cloned.1.call-start = ((), (), s32[]{:S(2)}) async-start(), calls=%async_computation.3 | async-start | bytes 4456448 | tf_op jit(solution)/shard_map/all_gather | solution.py:12
  9.0 124.4 %reduce-scatter.3.cloned.1.call-start = ((), (), s32[]{:S(2)}) async-start(), calls=%async_computation.4 | async-start | bytes 9175040 | tf_op jit(solution)/shard_map/reduce_scatter | solution.py:21
  59.3 122.7 %copy-start.1 = (bf16[128,896]{1,0:T(8,128)(2,1)S(1)}, bf16[128,896]{1,0:T(8,128)(2,1)}, u32[]{:S(2)}) copy-start(bf16[128,896]{1,0:T(8,128)(2,1)} %param.10) | copy-start | bytes 688132
  59.3 122.7 %copy-start.2 = (bf16[128,896]{1,0:T(8,128)(2,1)S(1)}, bf16[128,896]{1,0:T(8,128)(2,1)}, u32[]{:S(2)}) copy-start(bf16[128,896]{1,0:T(8,128)(2,1)} %param.9) | copy-start | bytes 688132
  59.3 267.7 %copy-start.5 = (bf16[512,896]{1,0:T(8,128)(2,1)S(1)}, bf16[512,896]{1,0:T(8,128)(2,1)}, u32[]{:S(2)}) copy-start(bf16[512,896]{1,0:T(8,128)(2,1)} %param.12) | copy-start | bytes 2752516
  59.3 122.7 %reduce-scatter.5.cloned.1.call-start = ((), (), s32[]{:S(2)}) async-start(), calls=%async_computation.5 | async-start | bytes 2293760 | tf_op jit(solution)/shard_map/reduce_scatter | solution.py:21
  133.5 193.6 %all-gather.5.cloned.1.call-start = ((), (), s32[]{:S(2)}) async-start(), calls=%async_computation.6 | async-start | bytes 11698176 | tf_op jit(solution)/shard_map/all_gather | solution.py:12
  184.2 147.4 %copy-start.6 = (bf16[512,896]{1,0:T(8,128)(2,1)S(1)}, bf16[512,896]{1,0:T(8,128)(2,1)}, u32[]{:S(2)}) copy-start(bf16[512,896]{1,0:T(8,128)(2,1)} %param.11) | copy-start | bytes 2752516
  327.0 5.2 %copy-start.3 = (bf16[2048,2688]{1,0:T(8,128)(2,1)S(1)}, bf16[2048,2688]{1,0:T(8,128)(2,1)}, u32[]{:S(2)}) copy-start(bf16[2048,2688]{1,0:T(8,128)(2,1)} %all-gather.5.cloned.1.call-done) | copy-start | bytes 33030148
  336.7 54.9 %all-to-all-start = ((f32[16,128,512]{2,1,0:T(8,128)}), f32[16,128,512]{2,1,0:T(8,128)}, u32[]{:S(2)}, u32[]{:S(2)}) async-start(f32[16,128,512]{2,1,0:T(8,128)} %bitcast.4), calls=%async_computation.2 | async-start | bytes 8388608 | tf_op jit(solution)/shard_map/all_to_all | solution.py:33
  350.4 3.5 copy-start.4
Sparse Core Ops, SparseCore 0:
  10.4 41.9 all-gather.2
  59.4 73.9 reduce-scatter.2
  136.0 45.9 reduce-scatter.4
  184.9 142.0 all-gather.4
where the time goes:
time: 404 us; the launch traced here: 401 us
  waiting for transfers between devices  341 us (84%)
  matrix products  29.5 us (7%)
  between operations  13.8 us (3%)
  other arithmetic  7.26 us (2%)
  starting transfers between devices  5.9 us (1%)
  local copies, waits for them, and re-layouts  4.2 us (1%)
    all_gather x2, waiting for transfers between devices, side_by_side(): lax.all_gather(both, axis, axis=dim, tiled=True)  186 us
    reduce_scatter x2, waiting for transfers between devices, own_rows(): subtotal = lax.psum_scatter(subtotal, axis, scatter_dimension=0, tiled=True)  123 us
    all_to_all x1, waiting for transfers between devices, sum_at_owner(): lax.all_to_all(blocks, axis, split_axis=0, concat_axis=0, tiled=True)  32 us
  transfers between devices with their start and end apart: 5, of which 5 were waited for; matrix products, arithmetic and copies ran while one was open for 4% of the time, Pallas kernels for 0%

commit v1 on v0

v1 whole, which is shorter than its diff:
```python
import jax
import jax.numpy as jnp
from jax import lax
from jax.experimental import pallas as pl
from jax.experimental.pallas import tpu as pltpu
from jax.sharding import PartitionSpec as P

MESH = pl.DeviceIdType.MESH
BF = jnp.bfloat16
F32 = jnp.float32
B = 128
H = B // 2
N_MSG = 176


def rows(ref, start, size):
    return ref.at[pl.ds(pl.multiple_of(start, H), size), :]


class Net:
    def __init__(self, send, recv, me):
        self.send_sem, self.recv_sem, self.me = send, recv, me
        self.count = 0
        self.sent = []

    def take(self, n):
        first = self.count
        self.count += n
        return first

    def copy(self, src, dst, msg, device):
        return pltpu.make_async_remote_copy(
            src_ref=src, dst_ref=dst, send_sem=self.send_sem.at[msg], recv_sem=self.recv_sem.at[msg],
            device_id=device, device_id_type=MESH,
        )

    def send(self, src, dst, msg, device):
        copy = self.copy(src, dst, msg, device)
        copy.start()
        self.sent.append(copy)

    def recv(self, dst, msg):
        self.copy(dst, dst, msg, self.me).wait_recv()

    def drain(self):
        for copy in self.sent:
            copy.wait_send()


class Ring:
    def __init__(self, net, buf, pos, device_of, slot_of):
        self.net, self.buf, self.pos, self.device_of, self.slot_of = net, buf, pos, device_of, slot_of
        self.right, self.far, self.left = (lax.rem(pos + n, 4) for n in (1, 2, 3))
        self.msg = net.take(4)

    def start(self, src=None):
        own = rows(self.buf, self.slot_of(self.pos), B)
        src = own if src is None else src
        self.net.send(src, own, self.msg, self.device_of(self.right))
        self.net.send(src, own, self.msg + 1, self.device_of(self.left))

    def from_left(self):
        slot = self.slot_of(self.left)
        self.net.recv(rows(self.buf, slot, B), self.msg)
        half = rows(self.buf, slot, H)
        self.net.send(half, half, self.msg + 2, self.device_of(self.right))

    def from_right(self):
        slot = self.slot_of(self.right)
        self.net.recv(rows(self.buf, slot, B), self.msg + 1)
        half = rows(self.buf, slot + H, H)
        self.net.send(half, half, self.msg + 3, self.device_of(self.left))

    def neighbours(self):
        self.from_left()
        self.from_right()

    def from_far(self):
        slot = self.slot_of(self.far)
        self.net.recv(rows(self.buf, slot, H), self.msg + 2)
        self.net.recv(rows(self.buf, slot + H, H), self.msg + 3)


def dot(a, b, dims):
    return lax.dot_general(a, b, (dims, ((), ())), preferred_element_type=F32)


def kernel(
    tok, go, gate, up, gw, uw, dw,
    gt_out, dgw, duw, ddw,
    go_all, tok_all, hid, gg, gu, part, s1, s2r, s2l, r1l, r1r, r2l, r2r,
    xs, zs1, zs2r, zs2l, zr1l, zr1r, zr2l, zr2r,
    gt_own, d2d_s, d2d_r, gt_s, gt_r, gt_acc,
    send_sem, recv_sem,
):
    row, col = lax.axis_index("row"), lax.axis_index("col")
    x, zh = lax.div(row, 4), lax.rem(row, 4)
    y, zl, k = lax.div(col, 4), lax.rem(lax.div(col, 2), 2), lax.rem(col, 2)
    net = Net(send_sem, recv_sem, (row, col))
    other = 1 - zl

    def x_dev(p):
        return (p * 4 + zh, col)

    def z_dev(p):
        return (x * 4 + p, col)

    def y_dev(p):
        return (row, p * 4 + zl * 2 + k)

    partner = (row, y * 4 + zl * 2 + 1 - k)
    across = (row, y * 4 + other * 2 + k)
    xr, xf, xl = (lax.rem(x + n, 4) for n in (1, 2, 3))
    zr, zf, zlft = (lax.rem(zh + n, 4) for n in (1, 2, 3))

    barrier = pltpu.get_barrier_semaphore()
    peers = [x_dev(xr), x_dev(xl), z_dev(zr), z_dev(zlft), partner, across]
    for dy in (1, 2, 3):
        p = lax.rem(y + dy, 4)
        peers += [(row, p * 4 + zl * 2 + k), (row, p * 4 + other * 2 + k)]
    for peer in peers:
        pl.semaphore_signal(barrier, inc=1, device_id=peer, device_id_type=MESH)
    pl.semaphore_wait(barrier, len(peers))

    class Column:
        def __init__(self, own, buf):
            self.own, self.buf = own, buf
            self.y0 = Ring(net, buf, y, y_dev, lambda p: (p * 4 + zl * 2 + k) * B)
            self.y1 = Ring(net, buf, y, y_dev, lambda p: (p * 4 + other * 2 + k) * B)
            self.m_across = net.take(1)
            self.m_pair = net.take(8)

        def slot(self, rel, flip, core):
            return (lax.rem(y + rel, 4) * 4 + (other if flip else zl) * 2 + core) * B

        def share(self, rel, flip, src=None):
            ref = rows(self.buf, self.slot(rel, flip, k), B)
            net.send(ref if src is None else src, ref, self.m_pair + rel * 2 + flip, partner)

        def start(self):
            mine = rows(self.buf, self.slot(0, 0, k), B)
            net.send(self.own, mine, self.m_across, across)
            self.y0.start(self.own)
            self.share(0, 0, self.own)
            mine[...] = self.own[...]

        def crossed(self):
            net.recv(rows(self.buf, self.slot(0, 1, k), B), self.m_across)
            self.y1.start()
            self.share(0, 1)

        def near(self, flip):
            ring = self.y1 if flip else self.y0
            ring.from_left()
            self.share(3, flip)
            ring.from_right()
            self.share(1, flip)

        def far(self, flip):
            (self.y1 if flip else self.y0).from_far()
            self.share(2, flip)

        def paired(self):
            for rel in (0, 3, 1, 2):
                for flip in (0, 1):
                    net.recv(rows(self.buf, self.slot(rel, flip, 1 - k), B), self.m_pair + rel * 2 + flip)

    class Gather:
        def __init__(self, buf):
            self.z = Ring(net, buf, zh, z_dev, lambda p: (x * 4 + p) * B)
            self.x = {}
            for back in (0, 1, 3, 2):
                at = lax.rem(zh + 4 - back, 4)
                self.x[back] = Ring(net, buf, x, x_dev, lambda p, at=at: (p * 4 + at) * B)

    col_go, col_tok = Column(go, go_all), Column(tok, tok_all)
    row_hid, row_gg, row_gu = Gather(hid), Gather(gg), Gather(gu)
    grads = (row_gg, row_gu)
    own = row * B

    col_go.start()

    def make_hidden(i, _):
        at = pl.ds(pl.multiple_of(i * 16, 16), 16)
        g, u = gate[at, :].astype(F32), up[at, :].astype(F32)
        hid[pl.ds(pl.multiple_of(own + i * 16, 16), 16), :] = (g * jax.nn.sigmoid(g) * u).astype(BF)
        return 0

    lax.fori_loop(0, B // 16, make_hidden, 0)
    row_hid.x[0].start()
    row_hid.z.start()

    col_go.crossed()
    col_go.near(0)
    col_go.near(1)
    row_hid.x[0].neighbours()
    col_go.far(0)
    col_go.far(1)
    col_go.paired()
    col_tok.start()

    nn = ((1,), (0,))

    def share_of(group):
        return dot(go_all[pl.ds(pl.multiple_of(group * 512, 512), 512), :], dw[...], nn)

    s1[...] = share_of(xf).astype(BF)
    order = (2, 1, 3, 0)
    dest = [lax.rem(zh + off, 4) for off in order]
    m1l, m1r, m2l, m2r = (net.take(4) for _ in range(4))
    for i, zb in enumerate(dest):
        net.send(rows(s1, zb * B, H), rows(r1l, i * H, H), m1l + i, x_dev(xr))
        net.send(rows(s1, zb * B + H, H), rows(r1r, i * H, H), m1r + i, x_dev(xl))
    for group in (xr, xl, x):
        part[pl.ds(pl.multiple_of(group * 512, 512), 512), :] = share_of(group)

    col_tok.crossed()
    for i, zb in enumerate(dest):
        lo, hi = pl.ds(i * B, H), pl.ds(i * B + H, H)
        base = (xr * 4 + zb) * B
        s2r[hi, :] = part[pl.ds(pl.multiple_of(base + H, H), H), :].astype(BF)
        net.recv(rows(r1l, i * H, H), m1l + i)
        s2r[lo, :] = (part[pl.ds(pl.multiple_of(base, H), H), :] + r1l[pl.ds(i * H, H), :].astype(F32)).astype(BF)
        net.send(rows(s2r, i * B, B), rows(r2l, i * B, B), m2l + i, x_dev(xr))
        base = (xl * 4 + zb) * B
        s2l[lo, :] = part[pl.ds(pl.multiple_of(base, H), H), :].astype(BF)
        net.recv(rows(r1r, i * H, H), m1r + i)
        s2l[hi, :] = (part[pl.ds(pl.multiple_of(base + H, H), H), :] + r1r[pl.ds(i * H, H), :].astype(F32)).astype(BF)
        net.send(rows(s2l, i * B, B), rows(r2r, i * B, B), m2r + i, x_dev(xl))
    col_tok.near(0)
    col_tok.near(1)
    col_tok.far(0)
    col_tok.far(1)

    def x_sum(i):
        net.recv(rows(r2l, i * B, B), m2l + i)
        net.recv(rows(r2r, i * B, B), m2r + i)
        base = (x * 4 + dest[i]) * B
        at = pl.ds(i * B, B)
        return part[pl.ds(pl.multiple_of(base, B), B), :] + r2l[at, :].astype(F32) + r2r[at, :].astype(F32)

    mz = net.take(4)
    zs1[...] = x_sum(0).astype(BF)
    net.send(zs1.at[pl.ds(0, H), :], zr1l, mz, z_dev(zr))
    net.send(zs1.at[pl.ds(H, H), :], zr1r, mz + 1, z_dev(zlft))
    row_hid.z.neighbours()
    xs[...] = x_sum(1)
    net.recv(zr1l, mz)
    zs2r[pl.ds(0, H), :] = (xs[pl.ds(0, H), :] + zr1l[...].astype(F32)).astype(BF)
    zs2r[pl.ds(H, H), :] = xs[pl.ds(H, H), :].astype(BF)
    net.send(zs2r, zr2l, mz + 2, z_dev(zr))
    xs[...] = x_sum(2)
    net.recv(zr1r, mz + 1)
    zs2l[pl.ds(H, H), :] = (xs[pl.ds(H, H), :] + zr1r[...].astype(F32)).astype(BF)
    zs2l[pl.ds(0, H), :] = xs[pl.ds(0, H), :].astype(BF)
    net.send(zs2l, zr2r, mz + 3, z_dev(zlft))
    xs[...] = x_sum(3)
    row_hid.x[1].start()
    row_hid.x[0].from_far()
    net.recv(zr2l, mz + 2)
    net.recv(zr2r, mz + 3)

    def make_grads(i, _):
        at = pl.ds(pl.multiple_of(i * 16, 16), 16)
        to = pl.ds(pl.multiple_of(own + i * 16, 16), 16)
        g, u = gate[at, :].astype(F32), up[at, :].astype(F32)
        gh = xs[at, :] + zr2l[at, :].astype(F32) + zr2r[at, :].astype(F32)
        s = jax.nn.sigmoid(g)
        gu[to, :] = (gh * (g * s)).astype(BF)
        gg[to, :] = (gh * u * s * (1.0 + g * (1.0 - s))).astype(BF)
        return 0

    lax.fori_loop(0, B // 16, make_grads, 0)
    for a in grads:
        a.x[0].start()
        a.z.start()

    nt = ((1,), (1,))
    m_d2d, m_gt = net.take(8), net.take(8)
    late = []

    def block_rows(ref, j):
        return rows(ref, j * B, B)

    def token_block(group, back):
        return group * 4 + lax.rem(zh + 4 - back, 4)

    def gt_share(j):
        q = lax.div(j, 2)
        at = pl.ds(pl.multiple_of(j * B, B), B)
        here = pl.ds(pl.multiple_of(q * B, B), B)
        mine = lax.rem(j, 2) == k
        value = dot(gg[at, :], gw[...], nt) + dot(gu[at, :], uw[...], nt)

        @pl.when(mine)
        def _():
            gt_own[here, :] = value

        @pl.when(jnp.logical_not(mine))
        def _():
            d2d_s[here, :] = value
            net.copy(block_rows(d2d_s, q), block_rows(d2d_r, q), m_d2d + q, partner).start()

    def gt_finish(j):
        q = lax.div(j, 2)
        here = pl.ds(pl.multiple_of(q * B, B), B)
        to_y, to_z = lax.div(j, 4), lax.rem(q, 2)
        m = lax.rem(to_y - y + 4, 4) * 2 + lax.rem(to_z - zl + 2, 2)

        @pl.when(lax.rem(j, 2) == k)
        def _():
            net.recv(block_rows(d2d_r, q), m_d2d + q)
            value = gt_own[here, :] + d2d_r[here, :]

            @pl.when(m == 0)
            def _():
                gt_acc[...] = value

            @pl.when(m != 0)
            def _():
                gt_s[pl.ds(pl.multiple_of(m * B, B), B), :] = value.astype(BF)
                net.copy(block_rows(gt_s, m), block_rows(gt_r, m), m_gt + m, (row, to_y * 4 + to_z * 2 + k)).start()

    def gt(*blocks):
        for j in blocks:
            gt_share(j)
        for j in blocks:
            gt_finish(j)

    tn = ((0,), (0,))

    def weights(group, out, left, right, first=False):
        at = pl.ds(pl.multiple_of(group * 512, 512), 512)
        value = dot(left[at, :], right[at, :], tn)
        if first:
            out[...] = value
        else:
            out[...] += value

    gt(token_block(x, 0))
    for a in grads:
        a.x[0].neighbours()
    row_hid.x[1].neighbours()
    row_hid.x[3].start()
    gt(token_block(xl, 0), token_block(xr, 0))
    for a in grads:
        a.z.from_left()
        a.x[1].start()
        a.z.from_right()
        a.x[3].start()
    gt(token_block(x, 1), token_block(x, 3))
    col_tok.paired()
    for a in grads:
        a.x[0].from_far()
    gt(token_block(xf, 0))
    row_hid.z.from_far()
    for a in grads:
        a.x[1].neighbours()
    gt(token_block(xl, 1), token_block(xr, 1))
    for a in grads:
        a.x[3].neighbours()
    gt(token_block(xl, 3), token_block(xr, 3))
    for a in grads:
        a.z.from_far()
        a.x[2].start()
    gt(token_block(x, 2))
    weights(x, dgw, tok_all, gg, True)
    weights(x, duw, tok_all, gu, True)
    weights(x, ddw, go_all, hid, True)
    row_hid.x[3].neighbours()
    row_hid.x[1].from_far()
    for a in grads:
        a.x[1].from_far()
    gt(token_block(xf, 1))
    for a in grads:
        a.x[3].from_far()
    gt(token_block(xf, 3))
    for a in grads:
        a.x[2].neighbours()
    row_hid.x[2].start()
    gt(token_block(xl, 2), token_block(xr, 2))
    for group in (xl, xr):
        weights(group, dgw, tok_all, gg)
        weights(group, duw, tok_all, gu)
    for a in grads:
        a.x[2].from_far()
    gt(token_block(xf, 2))
    weights(xf, dgw, tok_all, gg)
    weights(xf, duw, tok_all, gu)
    row_hid.x[2].neighbours()
    row_hid.x[3].from_far()
    weights(xl, ddw, go_all, hid)
    weights(xr, ddw, go_all, hid)
    row_hid.x[2].from_far()
    weights(xf, ddw, go_all, hid)

    total = gt_acc[...]
    for m in range(1, 8):
        net.recv(block_rows(gt_r, m), m_gt + m)
        total = total + gt_r[pl.ds(m * B, B), :].astype(F32)
    gt_out[...] = total.astype(BF)

    net.drain()
    for q in range(8):
        net.copy(block_rows(d2d_s, q), block_rows(d2d_r, q), m_d2d + q, partner).wait_send()
    for m in range(1, 8):
        net.copy(block_rows(gt_s, m), block_rows(gt_r, m), m_gt + m, partner).wait_send()
    assert net.count <= N_MSG, net.count


def per_device(tokens, grad_out, gate, up, gate_weight, up_weight, down_weight):
    f, d = gate.shape[1], tokens.shape[1]
    vmem = pl.BlockSpec(memory_space=pltpu.VMEM)
    return pl.pallas_call(
        kernel,
        name="swiglu_backward",
        out_shape=(
            jax.ShapeDtypeStruct((B, d), BF),
            jax.ShapeDtypeStruct((d, f), F32),
            jax.ShapeDtypeStruct((d, f), F32),
            jax.ShapeDtypeStruct((d, f), F32),
        ),
        in_specs=[vmem] * 7,
        out_specs=(vmem,) * 4,
        scratch_shapes=[
            pltpu.VMEM((16 * B, d), BF), pltpu.VMEM((16 * B, d), BF),
            pltpu.VMEM((16 * B, f), BF), pltpu.VMEM((16 * B, f), BF), pltpu.VMEM((16 * B, f), BF),
            pltpu.VMEM((16 * B, f), F32),
            pltpu.VMEM((4 * B, f), BF), pltpu.VMEM((4 * B, f), BF), pltpu.VMEM((4 * B, f), BF),
            pltpu.VMEM((4 * H, f), BF), pltpu.VMEM((4 * H, f), BF),
            pltpu.VMEM((4 * B, f), BF), pltpu.VMEM((4 * B, f), BF),
            pltpu.VMEM((B, f), F32),
            pltpu.VMEM((B, f), BF), pltpu.VMEM((B, f), BF), pltpu.VMEM((B, f), BF),
            pltpu.VMEM((H, f), BF), pltpu.VMEM((H, f), BF),
            pltpu.VMEM((B, f), BF), pltpu.VMEM((B, f), BF),
            pltpu.VMEM((8 * B, d), F32), pltpu.VMEM((8 * B, d), F32), pltpu.VMEM((8 * B, d), F32),
            pltpu.VMEM((8 * B, d), BF), pltpu.VMEM((8 * B, d), BF),
            pltpu.VMEM((B, d), F32),
            pltpu.SemaphoreType.DMA((N_MSG,)), pltpu.SemaphoreType.DMA((N_MSG,)),
        ],
        compiler_params=pltpu.CompilerParams(
            collective_id=0, has_side_effects=True, vmem_limit_bytes=67_000_000
        ),
    )(tokens, grad_out, gate, up, gate_weight, up_weight, down_weight)


def solution(mesh):
    act, wide = P("col", "row"), P("row", "col")
    return jax.shard_map(
        per_device,
        mesh=mesh,
        in_specs=(act, act, wide, wide, wide, wide, wide),
        out_specs=(act, wide, wide, wide),
        check_vma=False,
    )
```

time: 404 us -> 166 us (0.41)
  waiting for transfers between devices: 341 us -> 0 us
  Pallas kernels: 0 us -> 157 us
  matrix products: 29.5 us -> 0 us
  between operations: 13.8 us -> 0.65 us
  other arithmetic: 7.26 us -> 0 us
  starting transfers between devices: 5.9 us -> 0 us
    all_gather x2 -> x0, waiting for transfers between devices: 186 us -> none  [side_by_side(): lax.all_gather(both, axis, axis=dim, tiled=True)]
    pallas_call x0 -> x1, Pallas kernels: none -> 157 us  [per_device(): pl.pallas_call(kernel, name='swiglu_backward', out_shape=(jax.ShapeDtypeS...]
    reduce_scatter x2 -> x0, waiting for transfers between devices: 123 us -> none  [own_rows(): subtotal = lax.psum_scatter(subtotal, axis, scatter_dimension=0, tiled=True)]
    all_to_all x1 -> x0, waiting for transfers between devices: 32 us -> none  [sum_at_owner(): lax.all_to_all(blocks, axis, split_axis=0, concat_axis=0, tiled=True)]
    dot_general x5 -> x0, matrix products: 29.5 us -> none  [the longest x1 7.96 us: per_device(): lax.dot_general(tokens_all, stacked, outer, preferred_element_type=jnp.fl...]
    unnamed x14 -> x8, local copies, waits for them, and re-layouts: 2.1 us -> 7.94 us
    all_to_all x1 -> x0, starting transfers between devices: 5.74 us -> none  [sum_at_owner(): lax.all_to_all(blocks, axis, split_axis=0, concat_axis=0, tiled=True)]
  transfers between devices with their start and end apart: 5 -> 0, of which waited for: 5 -> 0; matrix products, arithmetic and copies ran while one was open for 4% -> 0% of each run, Pallas kernels for 0% -> 0%
where the time goes in v1:
time: 166 us; the launch traced here: 165 us
  Pallas kernels  157 us (95%)
  local copies, waits for them, and re-layouts  7.94 us (5%)
    pallas_call x1, Pallas kernels, per_device(): pl.pallas_call(kernel, name='swiglu_backward', out_shape=(jax.ShapeDtypeS...  157 us
    unnamed x8, local copies, waits for them, and re-layouts  7.94 us

profile of v1, /device:TPU:36, one launch (start us, length us, event | category | flops | bytes accessed | tf_op | source)
XLA Modules:
  0.0 165.4 jit_solution(1922988855008161865)
XLA Ops:
  0.6 156.8 %swiglu_backward.1 = (bf16[128,512]{1,0:T(8,128)(2,1)}, f32[512,896]{1,0:T(8,128)}, f32[512,896]{1,0:T(8,128)}, f32[512,896]{1,0:T(8,128)}) custom-call(bf16[128,512]{1,0:T(8,128)(2,1)} %tok.1, bf16[128,512]{1,0:T(8,128)(2,1)} %go.1, bf16[128,896]{1,0:T(8,128)(2,1)} %gate.1, bf16[128,896]{1,0:T(8,128)(2,1)} %up.1, bf16[512,896]{1,0:T(8,128)(2,1)} %gw.1, ...), custom_call_target="tpu_custom_call" | custom-call | tf_op jit(solution)/shard_map/swiglu_backward/pallas_call | solution.py:414
  157.4 1.6 copy.15
  159.0 0.0 copy-start.1
  159.0 3.0 %copy.16 = f32[512,896]{1,0:T(8,128)} copy(f32[512,896]{1,0:T(8,128)} %get-tuple-element.9) | data formatting | bytes 3670016
  162.0 0.0 copy-done.1
  162.0 0.0 copy-start
  162.0 1.2 copy.17
  163.2 0.9 copy-done
  164.2 1.2 copy.18
Async XLA Ops:
  159.0 3.0 %copy-start.1 = (f32[512,896]{1,0:T(8,128)S(1)}, f32[512,896]{1,0:T(8,128)}, u32[]{:S(2)}) copy-start(f32[512,896]{1,0:T(8,128)} %get-tuple-element.10) | copy-start | bytes 5505028
  162.0 2.2 %copy-start = (f32[512,896]{1,0:T(8,128)S(1)}, f32[512,896]{1,0:T(8,128)}, u32[]{:S(2)}) copy-start(f32[512,896]{1,0:T(8,128)} %get-tuple-element.11) | copy-start | bytes 5505028

commit v2 on v1

--- a/solution.py
+++ b/solution.py
@@ -11,6 +11,8 @@
 B = 128
 H = B // 2
 N_MSG = 176
+VMEM_LIMIT = 61_000_000
+FIRST = 384
 
 
 def rows(ref, start, size):
@@ -53,11 +55,10 @@
         self.right, self.far, self.left = (lax.rem(pos + n, 4) for n in (1, 2, 3))
         self.msg = net.take(4)
 
-    def start(self, src=None):
+    def start(self):
         own = rows(self.buf, self.slot_of(self.pos), B)
-        src = own if src is None else src
-        self.net.send(src, own, self.msg, self.device_of(self.right))
-        self.net.send(src, own, self.msg + 1, self.device_of(self.left))
+        self.net.send(own, own, self.msg, self.device_of(self.right))
+        self.net.send(own, own, self.msg + 1, self.device_of(self.left))
 
     def from_left(self):
         slot = self.slot_of(self.left)
@@ -86,12 +87,12 @@
 
 
 def kernel(
-    tok, go, gate, up, gw, uw, dw,
+    tok_in, go_in, gate_in, up_in, gw_in, uw_in, dw_in,
     gt_out, dgw, duw, ddw,
-    go_all, tok_all, hid, gg, gu, part, s1, s2r, s2l, r1l, r1r, r2l, r2r,
+    gw, uw, dw, go_all, tok_all, gwt, uwt, gate_a, gate_b, up, gh, hid, gg, gu, part, s1, s2r, s2l, r1l, r1r, r2l, r2r,
     xs, zs1, zs2r, zs2l, zr1l, zr1r, zr2l, zr2r,
     gt_own, d2d_s, d2d_r, gt_s, gt_r, gt_acc,
-    send_sem, recv_sem,
+    send_sem, recv_sem, load_sem,
 ):
     row, col = lax.axis_index("row"), lax.axis_index("col")
     x, zh = lax.div(row, 4), lax.rem(row, 4)
@@ -120,11 +121,26 @@
         peers += [(row, p * 4 + zl * 2 + k), (row, p * 4 + other * 2 + k)]
     for peer in peers:
         pl.semaphore_signal(barrier, inc=1, device_id=peer, device_id_type=MESH)
+
+    own = row * B
+    sources = [
+        (go_in, rows(go_all, col * B, B)),
+        (up_in, rows(up, own, B)),
+        (gate_in.at[:, pl.ds(FIRST, gate_in.shape[1] - FIRST)], rows(gate_b, own, B)),
+        (gate_in.at[:, pl.ds(0, FIRST)], rows(gate_a, own, B)),
+        (dw_in, dw),
+        (tok_in, rows(tok_all, col * B, B)),
+        (gw_in, gw),
+        (uw_in, uw),
+    ]
+    loads = [pltpu.make_async_copy(src, dst, load_sem.at[i]) for i, (src, dst) in enumerate(sources)]
+    for load in loads:
+        load.start()
     pl.semaphore_wait(barrier, len(peers))
 
     class Column:
-        def __init__(self, own, buf):
-            self.own, self.buf = own, buf
+        def __init__(self, buf):
+            self.buf = buf
             self.y0 = Ring(net, buf, y, y_dev, lambda p: (p * 4 + zl * 2 + k) * B)
             self.y1 = Ring(net, buf, y, y_dev, lambda p: (p * 4 + other * 2 + k) * B)
             self.m_across = net.take(1)
@@ -133,16 +149,15 @@
         def slot(self, rel, flip, core):
             return (lax.rem(y + rel, 4) * 4 + (other if flip else zl) * 2 + core) * B
 
-        def share(self, rel, flip, src=None):
+        def share(self, rel, flip):
             ref = rows(self.buf, self.slot(rel, flip, k), B)
-            net.send(ref if src is None else src, ref, self.m_pair + rel * 2 + flip, partner)
+            net.send(ref, ref, self.m_pair + rel * 2 + flip, partner)
 
         def start(self):
             mine = rows(self.buf, self.slot(0, 0, k), B)
-            net.send(self.own, mine, self.m_across, across)
-            self.y0.start(self.own)
-            self.share(0, 0, self.own)
-            mine[...] = self.own[...]
+            net.send(mine, mine, self.m_across, across)
+            self.y0.start()
+            self.share(0, 0)
 
         def crossed(self):
             net.recv(rows(self.buf, self.slot(0, 1, k), B), self.m_across)
@@ -173,31 +188,33 @@
                 at = lax.rem(zh + 4 - back, 4)
                 self.x[back] = Ring(net, buf, x, x_dev, lambda p, at=at: (p * 4 + at) * B)
 
-    col_go, col_tok = Column(go, go_all), Column(tok, tok_all)
-    row_hid, row_gg, row_gu = Gather(hid), Gather(gg), Gather(gu)
-    grads = (row_gg, row_gu)
-    own = row * B
-
+    col_go, col_tok = Column(go_all), Column(tok_all)
+    row_up, row_gb, row_gh = Gather(up), Gather(gate_b), Gather(gh)
+    ga_x = Ring(net, gate_a, x, x_dev, lambda p: (p * 4 + zh) * B)
+    ga_z, ga_zl, ga_zr, ga_zf = (
+        Ring(net, gate_a, zh, z_dev, lambda p, group=group: (group * 4 + p) * B) for group in (x, xl, xr, xf)
+    )
+
+    loads[0].wait()
     col_go.start()
-
-    def make_hidden(i, _):
-        at = pl.ds(pl.multiple_of(i * 16, 16), 16)
-        g, u = gate[at, :].astype(F32), up[at, :].astype(F32)
-        hid[pl.ds(pl.multiple_of(own + i * 16, 16), 16), :] = (g * jax.nn.sigmoid(g) * u).astype(BF)
-        return 0
-
-    lax.fori_loop(0, B // 16, make_hidden, 0)
-    row_hid.x[0].start()
-    row_hid.z.start()
-
+    loads[1].wait()
+    row_up.x[0].start()
+    loads[2].wait()
+    row_gb.x[0].start()
+    loads[3].wait()
+    ga_x.start()
     col_go.crossed()
+    row_up.z.start()
+    row_gb.z.start()
     col_go.near(0)
+    row_up.x[0].neighbours()
     col_go.near(1)
-    row_hid.x[0].neighbours()
+    row_gb.x[0].neighbours()
     col_go.far(0)
+    ga_x.neighbours()
     col_go.far(1)
+    loads[4].wait()
     col_go.paired()
-    col_tok.start()
 
     nn = ((1,), (0,))
 
@@ -214,7 +231,10 @@
     for group in (xr, xl, x):
         part[pl.ds(pl.multiple_of(group * 512, 512), 512), :] = share_of(group)
 
-    col_tok.crossed()
+    loads[5].wait()
+    col_tok.start()
+    row_up.z.neighbours()
+    ga_z.start()
     for i, zb in enumerate(dest):
         lo, hi = pl.ds(i * B, H), pl.ds(i * B + H, H)
         base = (xr * 4 + zb) * B
@@ -227,10 +247,10 @@
         net.recv(rows(r1r, i * H, H), m1r + i)
         s2l[hi, :] = (part[pl.ds(pl.multiple_of(base + H, H), H), :] + r1r[pl.ds(i * H, H), :].astype(F32)).astype(BF)
         net.send(rows(s2l, i * B, B), rows(r2r, i * B, B), m2r + i, x_dev(xl))
-    col_tok.near(0)
-    col_tok.near(1)
-    col_tok.far(0)
-    col_tok.far(1)
+        if i == 1:
+            row_gb.z.neighbours()
+    col_tok.crossed()
+    row_up.x[1].start()
 
     def x_sum(i):
         net.recv(rows(r2l, i * B, B), m2l + i)
@@ -239,45 +259,61 @@
         at = pl.ds(i * B, B)
         return part[pl.ds(pl.multiple_of(base, B), B), :] + r2l[at, :].astype(F32) + r2r[at, :].astype(F32)
 
-    mz = net.take(4)
+    mz = net.take(6)
+    lo, hi = pl.ds(0, H), pl.ds(H, H)
     zs1[...] = x_sum(0).astype(BF)
-    net.send(zs1.at[pl.ds(0, H), :], zr1l, mz, z_dev(zr))
-    net.send(zs1.at[pl.ds(H, H), :], zr1r, mz + 1, z_dev(zlft))
-    row_hid.z.neighbours()
+    net.send(zs1.at[lo, :], zr1l, mz, z_dev(zr))
+    net.send(zs1.at[hi, :], zr1r, mz + 1, z_dev(zlft))
+    col_tok.near(0)
+    row_up.x[3].start()
+    loads[6].wait()
+    loads[7].wait()
+    gwt[...] = gw[...].T
+    uwt[...] = uw[...].T
     xs[...] = x_sum(1)
+    zs2r[hi, :] = xs[hi, :].astype(BF)
+    net.send(zs2r.at[hi, :], zr2l.at[hi, :], mz + 2, z_dev(zr))
     net.recv(zr1l, mz)
-    zs2r[pl.ds(0, H), :] = (xs[pl.ds(0, H), :] + zr1l[...].astype(F32)).astype(BF)
-    zs2r[pl.ds(H, H), :] = xs[pl.ds(H, H), :].astype(BF)
-    net.send(zs2r, zr2l, mz + 2, z_dev(zr))
+    zs2r[lo, :] = (xs[lo, :] + zr1l[...].astype(F32)).astype(BF)
+    net.send(zs2r.at[lo, :], zr2l.at[lo, :], mz + 3, z_dev(zr))
     xs[...] = x_sum(2)
+    zs2l[lo, :] = xs[lo, :].astype(BF)
+    net.send(zs2l.at[lo, :], zr2r.at[lo, :], mz + 4, z_dev(zlft))
     net.recv(zr1r, mz + 1)
-    zs2l[pl.ds(H, H), :] = (xs[pl.ds(H, H), :] + zr1r[...].astype(F32)).astype(BF)
-    zs2l[pl.ds(0, H), :] = xs[pl.ds(0, H), :].astype(BF)
-    net.send(zs2l, zr2r, mz + 3, z_dev(zlft))
+    zs2l[hi, :] = (xs[hi, :] + zr1r[...].astype(F32)).astype(BF)
+    net.send(zs2l.at[hi, :], zr2r.at[hi, :], mz + 5, z_dev(zlft))
+    row_gb.x[1].start()
+    row_gb.x[3].start()
     xs[...] = x_sum(3)
-    row_hid.x[1].start()
-    row_hid.x[0].from_far()
-    net.recv(zr2l, mz + 2)
-    net.recv(zr2r, mz + 3)
-
-    def make_grads(i, _):
-        at = pl.ds(pl.multiple_of(i * 16, 16), 16)
-        to = pl.ds(pl.multiple_of(own + i * 16, 16), 16)
-        g, u = gate[at, :].astype(F32), up[at, :].astype(F32)
-        gh = xs[at, :] + zr2l[at, :].astype(F32) + zr2r[at, :].astype(F32)
-        s = jax.nn.sigmoid(g)
-        gu[to, :] = (gh * (g * s)).astype(BF)
-        gg[to, :] = (gh * u * s * (1.0 + g * (1.0 - s))).astype(BF)
-        return 0
-
-    lax.fori_loop(0, B // 16, make_grads, 0)
-    for a in grads:
-        a.x[0].start()
-        a.z.start()
-
-    nt = ((1,), (1,))
+    net.recv(zr2l.at[hi, :], mz + 2)
+    net.recv(zr2l.at[lo, :], mz + 3)
+    net.recv(zr2r.at[lo, :], mz + 4)
+    net.recv(zr2r.at[hi, :], mz + 5)
+
+    gh[pl.ds(pl.multiple_of(own, B), B), :] = (xs[...] + zr2l[...].astype(F32) + zr2r[...].astype(F32)).astype(BF)
+    row_gh.x[0].start()
+    row_gh.z.start()
+    ga_z.neighbours()
+    col_tok.near(1)
+
+    width = hid.shape[1]
+    parts = ((gate_a, pl.ds(0, FIRST)), (gate_b, pl.ds(FIRST, width - FIRST)))
+
+    def elementwise(j):
+        def some(i, _):
+            at = pl.ds(pl.multiple_of(j * B + i * 16, 16), 16)
+            for gate, cols in parts:
+                g, u, d = gate[at, :].astype(F32), up[at, cols].astype(F32), gh[at, cols].astype(F32)
+                s = jax.nn.sigmoid(g)
+                active = g * s
+                hid[at, cols] = (active * u).astype(BF)
+                gu[at, cols] = (d * active).astype(BF)
+                gg[at, cols] = (d * u * s * (1.0 + g * (1.0 - s))).astype(BF)
+            return 0
+
+        lax.fori_loop(0, B // 16, some, 0)
+
     m_d2d, m_gt = net.take(8), net.take(8)
-    late = []
 
     def block_rows(ref, j):
         return rows(ref, j * B, B)
@@ -290,7 +326,8 @@
         at = pl.ds(pl.multiple_of(j * B, B), B)
         here = pl.ds(pl.multiple_of(q * B, B), B)
         mine = lax.rem(j, 2) == k
-        value = dot(gg[at, :], gw[...], nt) + dot(gu[at, :], uw[...], nt)
+        elementwise(j)
+        value = dot(gg[at, :], gwt[...], nn) + dot(gu[at, :], uwt[...], nn)
 
         @pl.when(mine)
         def _():
@@ -337,61 +374,74 @@
         else:
             out[...] += value
 
+    def all_weights(group, first=False):
+        weights(group, dgw, tok_all, gg, first)
+        weights(group, duw, tok_all, gu, first)
+        weights(group, ddw, go_all, hid, first)
+
     gt(token_block(x, 0))
-    for a in grads:
-        a.x[0].neighbours()
-    row_hid.x[1].neighbours()
-    row_hid.x[3].start()
+    row_up.x[1].neighbours()
+    row_up.x[3].neighbours()
+    row_up.z.from_far()
+    row_gb.z.from_far()
+    row_up.x[2].start()
+    row_gh.z.from_left()
+    row_gh.x[1].start()
+    row_gh.z.from_right()
+    row_gh.x[3].start()
+    ga_zl.start()
+    row_gb.x[1].neighbours()
+    row_gb.x[3].neighbours()
+    row_gh.x[0].neighbours()
+    row_gb.x[2].start()
+    gt(token_block(x, 1), token_block(x, 3))
+    row_gh.z.from_far()
+    row_gh.x[2].start()
+    ga_zr.start()
     gt(token_block(xl, 0), token_block(xr, 0))
-    for a in grads:
-        a.z.from_left()
-        a.x[1].start()
-        a.z.from_right()
-        a.x[3].start()
-    gt(token_block(x, 1), token_block(x, 3))
+    ga_zl.neighbours()
+    ga_x.from_far()
+    ga_zf.start()
+    row_up.x[2].neighbours()
+    col_tok.far(0)
+    col_tok.far(1)
+    row_up.x[0].from_far()
+    row_gb.x[0].from_far()
+    row_gh.x[0].from_far()
+    gt(token_block(xf, 0))
+    ga_z.from_far()
+    gt(token_block(x, 2))
     col_tok.paired()
-    for a in grads:
-        a.x[0].from_far()
-    gt(token_block(xf, 0))
-    row_hid.z.from_far()
-    for a in grads:
-        a.x[1].neighbours()
+    ga_zr.neighbours()
+    row_gh.x[1].neighbours()
     gt(token_block(xl, 1), token_block(xr, 1))
-    for a in grads:
-        a.x[3].neighbours()
+    row_gb.x[2].neighbours()
+    all_weights(x, True)
+    row_gh.x[3].neighbours()
     gt(token_block(xl, 3), token_block(xr, 3))
-    for a in grads:
-        a.z.from_far()
-        a.x[2].start()
-    gt(token_block(x, 2))
-    weights(x, dgw, tok_all, gg, True)
-    weights(x, duw, tok_all, gu, True)
-    weights(x, ddw, go_all, hid, True)
-    row_hid.x[3].neighbours()
-    row_hid.x[1].from_far()
-    for a in grads:
+    ga_zf.neighbours()
+    for a in (row_up, row_gb):
         a.x[1].from_far()
+        a.x[3].from_far()
+    row_gh.x[2].neighbours()
+    ga_zl.from_far()
+    ga_zr.from_far()
+    gt(token_block(xl, 2), token_block(xr, 2))
+    row_gh.x[1].from_far()
     gt(token_block(xf, 1))
-    for a in grads:
-        a.x[3].from_far()
+    all_weights(xl)
+    row_gh.x[3].from_far()
     gt(token_block(xf, 3))
-    for a in grads:
-        a.x[2].neighbours()
-    row_hid.x[2].start()
-    gt(token_block(xl, 2), token_block(xr, 2))
-    for group in (xl, xr):
-        weights(group, dgw, tok_all, gg)
-        weights(group, duw, tok_all, gu)
-    for a in grads:
+    all_weights(xr)
+    for a in (row_up, row_gb):
         a.x[2].from_far()
-    gt(token_block(xf, 2))
+    ga_zf.from_far()
+    row_gh.x[2].from_far()
+    last = token_block(xf, 2)
+    gt_share(last)
     weights(xf, dgw, tok_all, gg)
+    gt_finish(last)
     weights(xf, duw, tok_all, gu)
-    row_hid.x[2].neighbours()
-    row_hid.x[3].from_far()
-    weights(xl, ddw, go_all, hid)
-    weights(xr, ddw, go_all, hid)
-    row_hid.x[2].from_far()
     weights(xf, ddw, go_all, hid)
 
     total = gt_acc[...]
@@ -408,22 +458,48 @@
     assert net.count <= N_MSG, net.count
 
 
+def hand_over(*results):
+    def body(*refs):
+        copies = [pltpu.make_async_copy(src, dst, refs[8].at[i]) for i, (src, dst) in enumerate(zip(refs[:4], refs[4:8]))]
+        for copy in copies:
+            copy.start()
+        for copy in copies:
+            copy.wait()
+
+    hbm = pl.BlockSpec(memory_space=pltpu.HBM)
+    vmem = pl.BlockSpec(memory_space=pltpu.VMEM)
+    return pl.pallas_call(
+        body,
+        name="hand_over",
+        in_specs=[vmem] * 4,
+        out_specs=(hbm,) * 4,
+        out_shape=tuple(jax.ShapeDtypeStruct(a.shape, a.dtype) for a in results),
+        scratch_shapes=[pltpu.SemaphoreType.DMA((4,))],
+        compiler_params=pltpu.CompilerParams(vmem_limit_bytes=16 * 1024 * 1024),
+    )(*results)
+
+
 def per_device(tokens, grad_out, gate, up, gate_weight, up_weight, down_weight):
     f, d = gate.shape[1], tokens.shape[1]
     vmem = pl.BlockSpec(memory_space=pltpu.VMEM)
-    return pl.pallas_call(
+    hbm = pl.BlockSpec(memory_space=pltpu.HBM)
+    results = pl.pallas_call(
         kernel,
         name="swiglu_backward",
         out_shape=(
-            jax.ShapeDtypeStruct((B, d), BF),
-            jax.ShapeDtypeStruct((d, f), F32),
-            jax.ShapeDtypeStruct((d, f), F32),
-            jax.ShapeDtypeStruct((d, f), F32),
+            pltpu.VMEM((B, d), BF),
+            pltpu.VMEM((d, f), F32),
+            pltpu.VMEM((d, f), F32),
+            pltpu.VMEM((d, f), F32),
         ),
-        in_specs=[vmem] * 7,
+        in_specs=[hbm] * 7,
         out_specs=(vmem,) * 4,
         scratch_shapes=[
+            pltpu.VMEM((d, f), BF), pltpu.VMEM((d, f), BF), pltpu.VMEM((d, f), BF),
             pltpu.VMEM((16 * B, d), BF), pltpu.VMEM((16 * B, d), BF),
+            pltpu.VMEM((f, d), BF), pltpu.VMEM((f, d), BF),
+            pltpu.VMEM((16 * B, FIRST), BF), pltpu.VMEM((16 * B, f - FIRST), BF),
+            pltpu.VMEM((16 * B, f), BF), pltpu.VMEM((16 * B, f), BF),
             pltpu.VMEM((16 * B, f), BF), pltpu.VMEM((16 * B, f), BF), pltpu.VMEM((16 * B, f), BF),
             pltpu.VMEM((16 * B, f), F32),
             pltpu.VMEM((4 * B, f), BF), pltpu.VMEM((4 * B, f), BF), pltpu.VMEM((4 * B, f), BF),
@@ -436,12 +512,13 @@
             pltpu.VMEM((8 * B, d), F32), pltpu.VMEM((8 * B, d), F32), pltpu.VMEM((8 * B, d), F32),
             pltpu.VMEM((8 * B, d), BF), pltpu.VMEM((8 * B, d), BF),
             pltpu.VMEM((B, d), F32),
-            pltpu.SemaphoreType.DMA((N_MSG,)), pltpu.SemaphoreType.DMA((N_MSG,)),
+            pltpu.SemaphoreType.DMA((N_MSG,)), pltpu.SemaphoreType.DMA((N_MSG,)), pltpu.SemaphoreType.DMA((8,)),
         ],
         compiler_params=pltpu.CompilerParams(
-            collective_id=0, has_side_effects=True, vmem_limit_bytes=67_000_000
+            collective_id=0, has_side_effects=True, vmem_limit_bytes=VMEM_LIMIT
         ),
     )(tokens, grad_out, gate, up, gate_weight, up_weight, down_weight)
+    return hand_over(*results)
 
 
 def solution(mesh):

time: 166 us -> 137 us (0.83)
  Pallas kernels: 157 us -> 135 us
  local copies, waits for them, and re-layouts: 7.94 us -> 0 us
    pallas_call x1 -> x2, Pallas kernels: 157 us -> 135 us  [the longest x1 133 us: per_device(): pl.pallas_call(kernel, name='swiglu_backward', out_shape=(pltpu.VMEM((B,...]
    unnamed x8 -> x0, local copies, waits for them, and re-layouts: 7.94 us -> none
where the time goes in v2:
time: 137 us; the launch traced here: 136 us
  Pallas kernels  135 us (99%)
    pallas_call x1, Pallas kernels, per_device(): pl.pallas_call(kernel, name='swiglu_backward', out_shape=(pltpu.VMEM((B,...  133 us

profile of v2, /device:TPU:36, one launch (start us, length us, event | category | flops | bytes accessed | tf_op | source)
XLA Modules:
  0.0 136.3 jit_solution(4009520643859180705)
XLA Ops:
  0.6 132.9 %swiglu_backward.1 = (bf16[128,512]{1,0:T(8,128)(2,1)S(1)}, f32[512,896]{1,0:T(8,128)S(1)}, f32[512,896]{1,0:T(8,128)S(1)}, f32[512,896]{1,0:T(8,128)S(1)}) custom-call(bf16[128,512]{1,0:T(8,128)(2,1)} %tok_in.1, bf16[128,512]{1,0:T(8,128)(2,1)} %go_in.1, bf16[128,896]{1,0:T(8,128)(2,1)} %gate_in.1, bf16[128,896]{1,0:T(8,128)(2,1)} %up_in.1, ...), custom_call_target="tpu_custom_call" | custom-call | tf_op jit(solution)/shard_map/swiglu_backward/pallas_call | solution.py:486
  133.6 2.5 %hand_over.1 = (bf16[128,512]{1,0:T(8,128)(2,1)}, f32[512,896]{1,0:T(8,128)}, f32[512,896]{1,0:T(8,128)}, f32[512,896]{1,0:T(8,128)}) custom-call(bf16[128,512]{1,0:T(8,128)(2,1)S(1)} %get-tuple-element.8.refs_0_, f32[512,896]{1,0:T(8,128)S(1)} %get-tuple-element.9.refs_1_, f32[512,896]{1,0:T(8,128)S(1)} %get-tuple-element.10.refs_2_, ...), custom_call_target="tpu_custom_call" | custom-call | tf_op jit(solution)/shard_map/hand_over/pallas_call | solution.py:471

commit v3 on v2

--- a/solution.py
+++ b/solution.py
@@ -12,7 +12,7 @@
 H = B // 2
 N_MSG = 176
 VMEM_LIMIT = 61_000_000
-FIRST = 384
+FIRST = 512
 
 
 def rows(ref, start, size):
@@ -50,31 +50,41 @@
 
 
 class Ring:
-    def __init__(self, net, buf, pos, device_of, slot_of):
+    def __init__(self, net, buf, pos, device_of, slot_of, split=False):
         self.net, self.buf, self.pos, self.device_of, self.slot_of = net, buf, pos, device_of, slot_of
         self.right, self.far, self.left = (lax.rem(pos + n, 4) for n in (1, 2, 3))
-        self.msg = net.take(4)
+        self.split = split
+        self.msg = net.take(6 if split else 4)
 
     def start(self):
-        own = rows(self.buf, self.slot_of(self.pos), B)
-        self.net.send(own, own, self.msg, self.device_of(self.right))
-        self.net.send(own, own, self.msg + 1, self.device_of(self.left))
+        slot = self.slot_of(self.pos)
+        first, second, own = rows(self.buf, slot, H), rows(self.buf, slot + H, H), rows(self.buf, slot, B)
+        right, left = self.device_of(self.right), self.device_of(self.left)
+        self.net.send(first if self.split else own, first if self.split else own, self.msg, right)
+        self.net.send(second if self.split else own, second if self.split else own, self.msg + 1, left)
+        if self.split:
+            self.net.send(second, second, self.msg + 4, right)
+            self.net.send(first, first, self.msg + 5, left)
 
     def from_left(self):
         slot = self.slot_of(self.left)
-        self.net.recv(rows(self.buf, slot, B), self.msg)
         half = rows(self.buf, slot, H)
+        self.net.recv(half if self.split else rows(self.buf, slot, B), self.msg)
         self.net.send(half, half, self.msg + 2, self.device_of(self.right))
 
     def from_right(self):
         slot = self.slot_of(self.right)
-        self.net.recv(rows(self.buf, slot, B), self.msg + 1)
         half = rows(self.buf, slot + H, H)
+        self.net.recv(half if self.split else rows(self.buf, slot, B), self.msg + 1)
         self.net.send(half, half, self.msg + 3, self.device_of(self.left))
 
     def neighbours(self):
         self.from_left()
         self.from_right()
+
+    def rest(self):
+        self.net.recv(rows(self.buf, self.slot_of(self.left) + H, H), self.msg + 4)
+        self.net.recv(rows(self.buf, self.slot_of(self.right), H), self.msg + 5)
 
     def from_far(self):
         slot = self.slot_of(self.far)
@@ -95,16 +105,20 @@
     send_sem, recv_sem, load_sem,
 ):
     row, col = lax.axis_index("row"), lax.axis_index("col")
-    x, zh = lax.div(row, 4), lax.rem(row, 4)
     y, zl, k = lax.div(col, 4), lax.rem(lax.div(col, 2), 2), lax.rem(col, 2)
+
+    def turned(p):
+        return p + zl * (3 - 2 * p)
+
+    x, zh = lax.div(row, 4), turned(lax.rem(row, 4))
     net = Net(send_sem, recv_sem, (row, col))
     other = 1 - zl
 
     def x_dev(p):
-        return (p * 4 + zh, col)
+        return (p * 4 + turned(zh), col)
 
     def z_dev(p):
-        return (x * 4 + p, col)
+        return (x * 4 + turned(p), col)
 
     def y_dev(p):
         return (row, p * 4 + zl * 2 + k)
@@ -181,18 +195,18 @@
                     net.recv(rows(self.buf, self.slot(rel, flip, 1 - k), B), self.m_pair + rel * 2 + flip)
 
     class Gather:
-        def __init__(self, buf):
-            self.z = Ring(net, buf, zh, z_dev, lambda p: (x * 4 + p) * B)
+        def __init__(self, buf, split=()):
+            self.z = Ring(net, buf, zh, z_dev, lambda p: (x * 4 + turned(p)) * B)
             self.x = {}
             for back in (0, 1, 3, 2):
-                at = lax.rem(zh + 4 - back, 4)
-                self.x[back] = Ring(net, buf, x, x_dev, lambda p, at=at: (p * 4 + at) * B)
+                at = turned(lax.rem(zh + 4 - back, 4))
+                self.x[back] = Ring(net, buf, x, x_dev, lambda p, at=at: (p * 4 + at) * B, back in split)
 
     col_go, col_tok = Column(go_all), Column(tok_all)
-    row_up, row_gb, row_gh = Gather(up), Gather(gate_b), Gather(gh)
-    ga_x = Ring(net, gate_a, x, x_dev, lambda p: (p * 4 + zh) * B)
+    row_up, row_gb, row_gh = Gather(up), Gather(gate_b), Gather(gh, (2,))
+    ga_x = Ring(net, gate_a, x, x_dev, lambda p: (p * 4 + turned(zh)) * B)
     ga_z, ga_zl, ga_zr, ga_zf = (
-        Ring(net, gate_a, zh, z_dev, lambda p, group=group: (group * 4 + p) * B) for group in (x, xl, xr, xf)
+        Ring(net, gate_a, zh, z_dev, lambda p, group=group: (group * 4 + turned(p)) * B) for group in (x, xl, xr, xf)
     )
 
     loads[0].wait()
@@ -223,7 +237,7 @@
 
     s1[...] = share_of(xf).astype(BF)
     order = (2, 1, 3, 0)
-    dest = [lax.rem(zh + off, 4) for off in order]
+    dest = [turned(lax.rem(zh + off, 4)) for off in order]
     m1l, m1r, m2l, m2r = (net.take(4) for _ in range(4))
     for i, zb in enumerate(dest):
         net.send(rows(s1, zb * B, H), rows(r1l, i * H, H), m1l + i, x_dev(xr))
@@ -319,7 +333,7 @@
         return rows(ref, j * B, B)
 
     def token_block(group, back):
-        return group * 4 + lax.rem(zh + 4 - back, 4)
+        return group * 4 + turned(lax.rem(zh + 4 - back, 4))
 
     def gt_share(j):
         q = lax.div(j, 2)
@@ -366,18 +380,17 @@
 
     tn = ((0,), (0,))
 
-    def weights(group, out, left, right, first=False):
-        at = pl.ds(pl.multiple_of(group * 512, 512), 512)
-        value = dot(left[at, :], right[at, :], tn)
-        if first:
-            out[...] = value
-        else:
-            out[...] += value
-
-    def all_weights(group, first=False):
-        weights(group, dgw, tok_all, gg, first)
-        weights(group, duw, tok_all, gu, first)
-        weights(group, ddw, go_all, hid, first)
+    early = lax.div(turned(zh), 2)
+    late = 1 - early
+
+    def weights(group, pair, first=False):
+        at = pl.ds(pl.multiple_of(group * 512 + pair * 256, 256), 256)
+        for out, left, right in ((dgw, tok_all, gg), (duw, tok_all, gu), (ddw, go_all, hid)):
+            value = dot(left[at, :], right[at, :], tn)
+            if first:
+                out[...] = value
+            else:
+                out[...] += value
 
     gt(token_block(x, 0))
     row_up.x[1].neighbours()
@@ -396,7 +409,6 @@
     row_gb.x[2].start()
     gt(token_block(x, 1), token_block(x, 3))
     row_gh.z.from_far()
-    row_gh.x[2].start()
     ga_zr.start()
     gt(token_block(xl, 0), token_block(xr, 0))
     ga_zl.neighbours()
@@ -407,42 +419,46 @@
     col_tok.far(1)
     row_up.x[0].from_far()
     row_gb.x[0].from_far()
-    row_gh.x[0].from_far()
-    gt(token_block(xf, 0))
     ga_z.from_far()
     gt(token_block(x, 2))
     col_tok.paired()
+    weights(x, early, True)
+    weights(x, late)
     ga_zr.neighbours()
     row_gh.x[1].neighbours()
     gt(token_block(xl, 1), token_block(xr, 1))
+    row_gh.x[3].neighbours()
+    row_gh.x[2].start()
+    gt(token_block(xl, 3), token_block(xr, 3))
+    weights(xl, early)
+    weights(xr, early)
+    row_gh.x[0].from_far()
+    gt(token_block(xf, 0))
     row_gb.x[2].neighbours()
-    all_weights(x, True)
-    row_gh.x[3].neighbours()
-    gt(token_block(xl, 3), token_block(xr, 3))
     ga_zf.neighbours()
     for a in (row_up, row_gb):
         a.x[1].from_far()
         a.x[3].from_far()
+    row_gh.x[1].from_far()
+    gt(token_block(xf, 1))
     row_gh.x[2].neighbours()
+    row_gh.x[3].from_far()
+    gt(token_block(xf, 3))
+    weights(xf, early)
+    row_gh.x[2].rest()
     ga_zl.from_far()
     ga_zr.from_far()
     gt(token_block(xl, 2), token_block(xr, 2))
-    row_gh.x[1].from_far()
-    gt(token_block(xf, 1))
-    all_weights(xl)
-    row_gh.x[3].from_far()
-    gt(token_block(xf, 3))
-    all_weights(xr)
     for a in (row_up, row_gb):
         a.x[2].from_far()
     ga_zf.from_far()
     row_gh.x[2].from_far()
     last = token_block(xf, 2)
     gt_share(last)
-    weights(xf, dgw, tok_all, gg)
+    weights(xl, late)
     gt_finish(last)
-    weights(xf, duw, tok_all, gu)
-    weights(xf, ddw, go_all, hid)
+    weights(xr, late)
+    weights(xf, late)
 
     total = gt_acc[...]
     for m in range(1, 8):

time: 137 us -> 133 us (0.971)
  Pallas kernels: 135 us -> 132 us
    pallas_call x1, Pallas kernels: 133 us -> 129 us  [per_device(): pl.pallas_call(kernel, name='swiglu_backward', out_shape=(pltpu.VMEM((B,...]
where the time goes in v3:
time: 133 us
  Pallas kernels  132 us (99%)
    pallas_call x1, Pallas kernels, per_device(): pl.pallas_call(kernel, name='swiglu_backward', out_shape=(pltpu.VMEM((B,...  129 us

profile of v3, /device:TPU:36, one launch (start us, length us, event | category | flops | bytes accessed | tf_op | source)
XLA Modules:
  0.0 132.6 jit_solution(13910060444176888352)
XLA Ops:
  0.6 129.3 %swiglu_backward.1 = (bf16[128,512]{1,0:T(8,128)(2,1)S(1)}, f32[512,896]{1,0:T(8,128)S(1)}, f32[512,896]{1,0:T(8,128)S(1)}, f32[512,896]{1,0:T(8,128)S(1)}) custom-call(bf16[128,512]{1,0:T(8,128)(2,1)} %tok_in.1, bf16[128,512]{1,0:T(8,128)(2,1)} %go_in.1, bf16[128,896]{1,0:T(8,128)(2,1)} %gate_in.1, bf16[128,896]{1,0:T(8,128)(2,1)} %up_in.1, ...), custom_call_target="tpu_custom_call" | custom-call | tf_op jit(solution)/shard_map/swiglu_backward/pallas_call | solution.py:502
  129.9 2.5 %hand_over.1 = (bf16[128,512]{1,0:T(8,128)(2,1)}, f32[512,896]{1,0:T(8,128)}, f32[512,896]{1,0:T(8,128)}, f32[512,896]{1,0:T(8,128)}) custom-call(bf16[128,512]{1,0:T(8,128)(2,1)S(1)} %get-tuple-element.8.refs_0_, f32[512,896]{1,0:T(8,128)S(1)} %get-tuple-element.9.refs_1_, f32[512,896]{1,0:T(8,128)S(1)} %get-tuple-element.10.refs_2_, ...), custom_call_target="tpu_custom_call" | custom-call | tf_op jit(solution)/shard_map/hand_over/pallas_call | solution.py:487

commit v4 on v3

--- a/solution.py
+++ b/solution.py
@@ -372,11 +372,18 @@
                 gt_s[pl.ds(pl.multiple_of(m * B, B), B), :] = value.astype(BF)
                 net.copy(block_rows(gt_s, m), block_rows(gt_r, m), m_gt + m, (row, to_y * 4 + to_z * 2 + k)).start()
 
+    waiting = []
+
+    def flush():
+        for j in waiting:
+            gt_finish(j)
+        waiting.clear()
+
     def gt(*blocks):
         for j in blocks:
             gt_share(j)
-        for j in blocks:
-            gt_finish(j)
+        flush()
+        waiting.extend(blocks)
 
     tn = ((0,), (0,))
 
@@ -408,57 +415,66 @@
     row_gh.x[0].neighbours()
     row_gb.x[2].start()
     gt(token_block(x, 1), token_block(x, 3))
-    row_gh.z.from_far()
     ga_zr.start()
     gt(token_block(xl, 0), token_block(xr, 0))
-    ga_zl.neighbours()
-    ga_x.from_far()
-    ga_zf.start()
     row_up.x[2].neighbours()
     col_tok.far(0)
     col_tok.far(1)
-    row_up.x[0].from_far()
-    row_gb.x[0].from_far()
+    row_gh.z.from_far()
     ga_z.from_far()
     gt(token_block(x, 2))
+    ga_x.from_far()
+    ga_zl.neighbours()
+    ga_zf.start()
     col_tok.paired()
     weights(x, early, True)
     weights(x, late)
-    ga_zr.neighbours()
+    row_up.x[0].from_far()
+    row_gb.x[0].from_far()
     row_gh.x[1].neighbours()
-    gt(token_block(xl, 1), token_block(xr, 1))
     row_gh.x[3].neighbours()
     row_gh.x[2].start()
-    gt(token_block(xl, 3), token_block(xr, 3))
+    gt(token_block(xl, 1), token_block(xl, 3))
     weights(xl, early)
+    ga_zr.neighbours()
+    gt(token_block(xr, 1), token_block(xr, 3))
     weights(xr, early)
+    row_gb.x[2].neighbours()
     row_gh.x[0].from_far()
     gt(token_block(xf, 0))
-    row_gb.x[2].neighbours()
     ga_zf.neighbours()
     for a in (row_up, row_gb):
         a.x[1].from_far()
         a.x[3].from_far()
     row_gh.x[1].from_far()
     gt(token_block(xf, 1))
+    flush()
     row_gh.x[2].neighbours()
     row_gh.x[3].from_far()
     gt(token_block(xf, 3))
     weights(xf, early)
+    flush()
     row_gh.x[2].rest()
     ga_zl.from_far()
     ga_zr.from_far()
     gt(token_block(xl, 2), token_block(xr, 2))
+    flush()
     for a in (row_up, row_gb):
         a.x[2].from_far()
     ga_zf.from_far()
     row_gh.x[2].from_far()
     last = token_block(xf, 2)
     gt_share(last)
+    gt_finish(last)
     weights(xl, late)
-    gt_finish(last)
     weights(xr, late)
     weights(xf, late)
+
+    net.drain()
+    for q in range(8):
+        net.copy(block_rows(d2d_s, q), block_rows(d2d_r, q), m_d2d + q, partner).wait_send()
+    for m in range(1, 8):
+        net.copy(block_rows(gt_s, m), block_rows(gt_r, m), m_gt + m, partner).wait_send()
 
     total = gt_acc[...]
     for m in range(1, 8):
@@ -466,11 +482,6 @@
         total = total + gt_r[pl.ds(m * B, B), :].astype(F32)
     gt_out[...] = total.astype(BF)
 
-    net.drain()
-    for q in range(8):
-        net.copy(block_rows(d2d_s, q), block_rows(d2d_r, q), m_d2d + q, partner).wait_send()
-    for m in range(1, 8):
-        net.copy(block_rows(gt_s, m), block_rows(gt_r, m), m_gt + m, partner).wait_send()
     assert net.count <= N_MSG, net.count
 
 

time: 133 us -> 132 us (level)
  no operation moved by 1% of the time
where the time goes in v4:
time: 132 us
  Pallas kernels  131 us (99%)
    pallas_call x1, Pallas kernels, per_device(): pl.pallas_call(kernel, name='swiglu_backward', out_shape=(pltpu.VMEM((B,...  129 us

profile of v4, /device:TPU:36, one launch (start us, length us, event | category | flops | bytes accessed | tf_op | source)
XLA Modules:
  0.0 132.2 jit_solution(13161171149539880803)
XLA Ops:
  0.6 128.9 %swiglu_backward.1 = (bf16[128,512]{1,0:T(8,128)(2,1)S(1)}, f32[512,896]{1,0:T(8,128)S(1)}, f32[512,896]{1,0:T(8,128)S(1)}, f32[512,896]{1,0:T(8,128)S(1)}) custom-call(bf16[128,512]{1,0:T(8,128)(2,1)} %tok_in.1, bf16[128,512]{1,0:T(8,128)(2,1)} %go_in.1, bf16[128,896]{1,0:T(8,128)(2,1)} %gate_in.1, bf16[128,896]{1,0:T(8,128)(2,1)} %up_in.1, ...), custom_call_target="tpu_custom_call" | custom-call | tf_op jit(solution)/shard_map/swiglu_backward/pallas_call | solution.py:513
  129.5 2.5 %hand_over.1 = (bf16[128,512]{1,0:T(8,128)(2,1)}, f32[512,896]{1,0:T(8,128)}, f32[512,896]{1,0:T(8,128)}, f32[512,896]{1,0:T(8,128)}) custom-call(bf16[128,512]{1,0:T(8,128)(2,1)S(1)} %get-tuple-element.8.refs_0_, f32[512,896]{1,0:T(8,128)S(1)} %get-tuple-element.9.refs_1_, f32[512,896]{1,0:T(8,128)S(1)} %get-tuple-element.10.refs_2_, ...), custom_call_target="tpu_custom_call" | custom-call | tf_op jit(solution)/shard_map/hand_over/pallas_call | solution.py:498

commit v5 on v4

--- a/solution.py
+++ b/solution.py
@@ -246,9 +246,9 @@
         part[pl.ds(pl.multiple_of(group * 512, 512), 512), :] = share_of(group)
 
     loads[5].wait()
-    col_tok.start()
     row_up.z.neighbours()
     ga_z.start()
+    col_tok.start()
     for i, zb in enumerate(dest):
         lo, hi = pl.ds(i * B, H), pl.ds(i * B + H, H)
         base = (xr * 4 + zb) * B
@@ -263,7 +263,6 @@
         net.send(rows(s2l, i * B, B), rows(r2r, i * B, B), m2r + i, x_dev(xl))
         if i == 1:
             row_gb.z.neighbours()
-    col_tok.crossed()
     row_up.x[1].start()
 
     def x_sum(i):
@@ -278,8 +277,9 @@
     zs1[...] = x_sum(0).astype(BF)
     net.send(zs1.at[lo, :], zr1l, mz, z_dev(zr))
     net.send(zs1.at[hi, :], zr1r, mz + 1, z_dev(zlft))
+    row_up.x[3].start()
+    col_tok.crossed()
     col_tok.near(0)
-    row_up.x[3].start()
     loads[6].wait()
     loads[7].wait()
     gwt[...] = gw[...].T

time: 132 us -> 132 us (level)
  no operation moved by 1% of the time
where the time goes in v5:
time: 132 us
  Pallas kernels  131 us (99%)
    pallas_call x1, Pallas kernels, per_device(): pl.pallas_call(kernel, name='swiglu_backward', out_shape=(pltpu.VMEM((B,...  129 us

profile of v5, /device:TPU:36, one launch (start us, length us, event | category | flops | bytes accessed | tf_op | source)
XLA Modules:
  0.0 132.0 jit_solution(17103282399213968093)
XLA Ops:
  0.6 128.7 %swiglu_backward.1 = (bf16[128,512]{1,0:T(8,128)(2,1)S(1)}, f32[512,896]{1,0:T(8,128)S(1)}, f32[512,896]{1,0:T(8,128)S(1)}, f32[512,896]{1,0:T(8,128)S(1)}) custom-call(bf16[128,512]{1,0:T(8,128)(2,1)} %tok_in.1, bf16[128,512]{1,0:T(8,128)(2,1)} %go_in.1, bf16[128,896]{1,0:T(8,128)(2,1)} %gate_in.1, bf16[128,896]{1,0:T(8,128)(2,1)} %up_in.1, ...), custom_call_target="tpu_custom_call" | custom-call | tf_op jit(solution)/shard_map/swiglu_backward/pallas_call | solution.py:513
  129.3 2.5 %hand_over.1 = (bf16[128,512]{1,0:T(8,128)(2,1)}, f32[512,896]{1,0:T(8,128)}, f32[512,896]{1,0:T(8,128)}, f32[512,896]{1,0:T(8,128)}) custom-call(bf16[128,512]{1,0:T(8,128)(2,1)S(1)} %get-tuple-element.8.refs_0_, f32[512,896]{1,0:T(8,128)S(1)} %get-tuple-element.9.refs_1_, f32[512,896]{1,0:T(8,128)S(1)} %get-tuple-element.10.refs_2_, ...), custom_call_target="tpu_custom_call" | custom-call | tf_op jit(solution)/shard_map/hand_over/pallas_call | solution.py:498
